TPU v7x, 128 devices: a whole 4x4x4 slice. The times are simulated.
128 devices in a mesh: layer: 8 (over z_lo, y), lat: 16 (over x, z_hi, core).
Axes of the slice: x: 4, y: 4, z: 4 (z_hi: 2, z_lo: 2; z = z_hi * 2 + z_lo), core: 2. Of those that a mesh axis runs over, the one named last changes fastest.
Arguments:
- activations: bfloat16 [8, 512, 2048], P(None, None, 'layer'), may hold values from -6 to 6
- targets: bfloat16 [8, 512, 2048], P(None, None, 'layer'), may hold values from -6 to 6
- encoder: bfloat16 [8, 2048, 8192], P(None, 'layer', 'lat'), may hold values from -0.125 to 0.125
- bias: float32 [8, 8192], P(None, 'lat'), may hold values from -3 to 3
- decoder: bfloat16 [36, 8192, 2048], P(None, 'lat', 'layer'), may hold values from -0.75 to 0.75
- active: int32 [8, 512, 64], replicated, may hold values from 0 to 8191, all different within a row
Outputs:
- grad_encoder: bfloat16 [8, 2048, 8192], P(None, 'layer', 'lat')
- grad_bias: float32 [8, 8192], P(None, 'lat')
- grad_decoder: bfloat16 [36, 8192, 2048], P(None, 'lat', 'layer')
Inputs may be any that keep to these rules, and one draw needn't show every extreme that they name: `active`: each row names 64 different latents.
All inputs are finite; a program needn't handle non-finite values.
Results may differ from a plain program's by a relative error of at most 0.0064.
Values may be sent and summed in bfloat16 or wider, within the bound.
No kernel may reach another device: no remote copies, remote signals or barrier semaphores. Data moves between devices by JAX's collectives and lax.ppermute only.
A program may use at most 128 MiB of HBM per device.

v0:
```python
import jax
import jax.numpy as jnp
from jax import lax
from jax.sharding import PartitionSpec as P

LAYERS = 8


def padded_to(lines, size):
    spare = -len(lines) % size
    return jnp.pad(lines, [(0, spare)] + [(0, 0)] * (lines.ndim - 1))


def sum_by_parts(x, axis):
    lines = x.reshape(-1, *x.shape[1:][-1:])
    own = lax.psum_scatter(
        padded_to(lines, lax.axis_size(axis)), axis, scatter_dimension=0, tiled=True
    )
    whole = lax.all_gather(own, axis).reshape(-1, *lines.shape[1:])
    return lax.slice_in_dim(whole, 0, len(lines)).reshape(x.shape)


def pair_index(source, target):
    return source * LAYERS - source * (source - 1) // 2 + (target - source)


def on_device(activations, targets, encoder, bias, decoder, active):
    lat_width = encoder.shape[2]
    first = lax.axis_index("lat") * lat_width
    columns = first + jnp.arange(lat_width, dtype=jnp.int32)
    masks = jnp.stack(
        [
            jnp.any(active[source][:, :, None] == columns[None, None, :], axis=1)
            for source in range(LAYERS)
        ]
    ).astype(jnp.float32)
    partial_value = jnp.einsum(
        "ltd,ldf->ltf", activations, encoder, preferred_element_type=jnp.float32
    )
    preact = lax.psum(partial_value, "layer") + bias[:, None, :]
    latent_act = (preact * masks).astype(jnp.bfloat16)
    rebuilt_list = []
    for target in range(LAYERS):
        summed = jnp.dot(
            latent_act[0], decoder[pair_index(0, target)], preferred_element_type=jnp.float32
        )
        for source in range(1, target + 1):
            summed = summed + jnp.dot(
                latent_act[source],
                decoder[pair_index(source, target)],
                preferred_element_type=jnp.float32,
            )
        rebuilt_list.append(summed)
    rebuilt = jnp.stack(rebuilt_list)
    complete = lax.psum(rebuilt, "lat")
    errors = (complete - targets.astype(jnp.float32)).astype(jnp.bfloat16)
    by_tokens = (((0,), (0,)), ((), ()))
    by_width = (((1,), (1,)), ((), ()))
    grad_pairs = []
    for source in range(LAYERS):
        for target in range(source, LAYERS):
            grad_pairs.append(
                lax.dot_general(
                    latent_act[source],
                    errors[target],
                    by_tokens,
                    preferred_element_type=jnp.float32,
                ).astype(jnp.bfloat16)
            )
    grad_decoder = jnp.stack(grad_pairs)
    grad_list = []
    for source in range(LAYERS):
        summed = lax.dot_general(
            errors[source],
            decoder[pair_index(source, source)],
            by_width,
            preferred_element_type=jnp.float32,
        )
        for target in range(source + 1, LAYERS):
            summed = summed + lax.dot_general(
                errors[target],
                decoder[pair_index(source, target)],
                by_width,
                preferred_element_type=jnp.float32,
            )
        grad_list.append(summed)
    grad_partial = jnp.stack(grad_list)
    grad_act = sum_by_parts(grad_partial, "layer")
    grad_pre = (grad_act * masks).astype(jnp.bfloat16)
    grad_encoder = jnp.einsum(
        "ltd,ltf->ldf", activations, grad_pre, preferred_element_type=jnp.float32
    ).astype(jnp.bfloat16)
    grad_bias = jnp.sum(grad_pre.astype(jnp.float32), axis=1)
    return (grad_encoder, grad_bias, grad_decoder)


def solution(mesh):
    placed = (
        P(None, None, "layer"),
        P(None, None, "layer"),
        P(None, "layer", "lat"),
        P(None, "lat"),
        P(None, "lat", "layer"),
        P(),
    )
    return jax.shard_map(
        on_device,
        mesh=mesh,
        in_specs=placed,
        out_specs=(P(None, "layer", "lat"), P(None, "lat"), P(None, "lat", "layer")),
        check_vma=False,
    )
```

profile of v0, /device:TPU:1, one launch (start us, length us, event | category | flops | bytes accessed | tf_op | source)
XLA Modules:
  0.0 620.0 jit_solution(13394112168313899540)
XLA Ops:
  7.2 1.5 copy-done
  8.8 6.2 %fusion.261 = f32[8,512,512]{2,1,0:T(8,128)} fusion(bf16[8,512,256]{2,1,0:T(8,128)(2,1)S(1)} %copy-done, bf16[8,256,512]{2,1,0:T(8,128)(2,1)} %param.8), kind=kOutput, calls=%fused_computation.401 | convolution fusion | flops 1073741824 | bytes 12582912 | tf_op jit(solution)/shard_map/ltd,ldf->ltf/dot_general | solution.py:37
  15.1 1.1 copy-done.6
  18.3 1.7 copy.21
  20.0 1.8 copy.22
  21.8 1.7 copy.23
  23.5 1.8 copy.24
  25.3 1.7 copy.25
  27.9 141.9 %compare_reduce_fusion = (pred[512,512]{1,0:T(8,128)(4,1)S(1)}, pred[512,512]{1,0:T(8,128)(4,1)}, pred[512,512]{1,0:T(8,128)(4,1)}, pred[512,512]{1,0:T(8,128)(4...) fusion(s32[512,64]{1,0:T(8,128)S(1)} %copy.26, ...), kind=kLoop, calls=%fused_computation | loop fusion | flops 266338304 | bytes 3147776 | tf_op jit(solution)/shard_map/reduce_or | solution.py:33
  169.8 1.7 bitcast_dynamic-update-slice_fusion.7
  171.5 1.7 bitcast_dynamic-update-slice_fusion.6
  173.1 1.7 bitcast_dynamic-update-slice_fusion.5
  174.8 1.7 bitcast_dynamic-update-slice_fusion.4
  176.5 1.7 bitcast_dynamic-update-slice_fusion.3
  180.3 22.3 %all-reduce.3.cloned.1.call-done = f32[8,512,512]{2,1,0:T(8,128)} async-done(((f32[8,512,512]{2,1,0:T(8,128)}), f32[8,512,512]{2,1,0:T(8,128)}) %all-reduce.3.cloned.1.call-update) | async-done | bytes 8388624 | tf_op jit(solution)/shard_map/psum | solution.py:40
  202.6 5.9 select_convert_fusion.1
  208.6 2.3 fusion.15
  210.9 1.2 fusion.183
  212.1 1.2 fusion.177
  213.4 1.2 fusion.169
  214.6 1.2 fusion.159
  215.9 1.2 fusion.147
  224.2 1.1 fusion.29
  225.3 1.1 fusion.27
  226.3 1.1 fusion.25
  227.4 1.1 fusion.23
  228.5 1.1 fusion.21
  229.6 1.1 fusion.19
  230.7 1.1 fusion.17
  232.1 150.0 %all-reduce.5.cloned.1.call-done = f32[8,512,256]{2,1,0:T(8,128)} async-done(((f32[8,512,256]{2,1,0:T(8,128)}), f32[8,512,256]{2,1,0:T(8,128)}) %all-reduce.5.cloned.1.call-update) | async-done | bytes 4194320 | tf_op jit(solution)/shard_map/psum | solution.py:55
  382.1 3.5 subtract_convert_fusion
  385.6 2.8 fusion.185
  388.4 1.3 fusion.179
  389.7 1.4 fusion.171
  391.1 1.3 fusion.161
  392.3 1.3 fusion.149
  393.6 1.3 fusion.135
  394.9 1.3 fusion.119
  406.0 3.4 copy-done.5
  409.7 94.0 %reduce-scatter.2.cloned.1.call-done = f32[512,512]{1,0:T(8,128)} async-done(((f32[4096,512]{1,0:T(8,128)}), f32[512,512]{1,0:T(8,128)}) %reduce-scatter.2.cloned.1.call-update) | async-done | bytes 1048592 | tf_op jit(solution)/shard_map/reduce_scatter | solution.py:16
  503.8 2.3 fusion.31
  506.1 2.2 fusion.33
  508.2 2.2 fusion.35
  510.4 2.0 fusion.37
  513.4 1.1 fusion.41
  514.5 1.1 fusion.43
  515.6 1.1 fusion.45
  519.8 1.1 fusion.53
  520.8 1.1 fusion.55
  521.9 1.1 fusion.57
  526.1 1.1 fusion.65
  527.1 1.1 fusion.67
  528.2 1.1 fusion.69
  532.4 1.1 fusion.77
  533.4 1.1 fusion.79
  534.5 1.1 fusion.81
  538.7 1.1 fusion.89
  539.7 1.1 fusion.91
  540.8 1.1 fusion.93
  545.0 1.1 fusion.101
  546.0 49.8 %all-gather.3.cloned.1.call-done = f32[4096,512]{1,0:T(8,128)} async-done(((f32[512,512]{1,0:T(8,128)}), f32[4096,512]{1,0:T(8,128)}) %all-gather.3.cloned.1.call-update) | async-done | bytes 8388624 | tf_op jit(solution)/shard_map/all_gather | solution.py:19
  595.8 7.5 %convert_bitcast_fusion = bf16[8,256,512]{1,2,0:T(8,128)(2,1)} fusion(bf16[8,512,256]{2,1,0:T(8,128)(2,1)S(1)} %copy-done, pred[8,512,512]{2,1,0:T(8,128)(4,1)} %bitcast_dynamic-update-slice_fusion, f32[8,512,512]{2,1,0:T(8,128)} %bitcast.608), kind=kOutput, calls=%fused_computation.12 | convolution fusion | flops 1076887552 | bytes 14680064 | tf_op jit(solution)/shard_map/ltd,ltf->ldf/dot_general | solution.py:90
  603.3 3.9 copy.28
  607.2 6.0 convert_reduce_fusion
  (111 shorter events, 38.8 us)
Async XLA Ops:
  7.2 1.6 copy-start
  7.2 195.4 %all-reduce.3.cloned.1.call-start = ((), (), s32[]{:S(2)}) async-start(), calls=%async_computation.1 | async-start | bytes 16777216 | tf_op jit(solution)/shard_map/psum | solution.py:40
  15.0 1.2 copy-start.6
  15.0 367.0 %all-reduce.5.cloned.1.call-start = ((), (), s32[]{:S(2)}) async-start(), calls=%async_computation.2 | async-start | bytes 8388608 | tf_op jit(solution)/shard_map/psum | solution.py:55
  27.9 174.7 %copy-start.7 = (f32[8,512]{1,0:T(8,128)S(1)}, f32[8,512]{1,0:T(8,128)}, u32[]{:S(2)}) copy-start(f32[8,512]{1,0:T(8,128)} %param.9) | copy-start | bytes 49156
  202.6 14.6 %slice-start = ((s8[9437184]{0:T(1024)(128)(4,1)}), s8[4194304]{0:T(1024)(128)(4,1)S(1)}, s32[]{:S(2)}) async-start(s8[9437184]{0:T(1024)(128)(4,1)} %bitcast.604), calls=%async_computation.5 | async-start | bytes 8388608
  202.6 14.6 %slice-start.1 = ((s8[9437184]{0:T(1024)(128)(4,1)}), s8[4194304]{0:T(1024)(128)(4,1)S(1)}, s32[]{:S(2)}) async-start(s8[9437184]{0:T(1024)(128)(4,1)} %bitcast.604), calls=%async_computation.6 | async-start | bytes 8388608
  208.5 22.2 %copy-start.1 = (bf16[8,512,512]{2,1,0:T(8,128)(2,1)}, bf16[8,512,512]{2,1,0:T(8,128)(2,1)S(1)}, u32[]{:S(2)}) copy-start(bf16[8,512,512]{2,1,0:T(8,128)(2,1)S(1)} %select_convert_fusion.1) | copy-start | bytes 12582916
  208.6 8.6 %slice-start.2 = ((s8[9437184]{0:T(1024)(128)(4,1)}), s8[1048576]{0:T(1024)(128)(4,1)S(1)}, s32[]{:S(2)}) async-start(s8[9437184]{0:T(1024)(128)(4,1)} %bitcast.604), calls=%async_computation.7 | async-start | bytes 2097152
  231.8 271.9 %reduce-scatter.2.cloned.1.call-start = ((), (), s32[]{:S(2)}) async-start(), calls=%async_computation.3 | async-start | bytes 9437184 | tf_op jit(solution)/shard_map/reduce_scatter | solution.py:16
  382.1 14.1 %slice-start.3 = ((s8[9437184]{0:T(1024)(128)(4,1)}), s8[4194304]{0:T(1024)(128)(4,1)S(1)}, s32[]{:S(2)}) async-start(s8[9437184]{0:T(1024)(128)(4,1)} %bitcast.606), calls=%async_computation.8 | async-start | bytes 8388608
  382.1 14.2 %slice-start.4 = ((s8[9437184]{0:T(1024)(128)(4,1)}), s8[4194304]{0:T(1024)(128)(4,1)S(1)}, s32[]{:S(2)}) async-start(s8[9437184]{0:T(1024)(128)(4,1)} %bitcast.606), calls=%async_computation.9 | async-start | bytes 8388608
  385.6 20.1 %copy-start.3 = (bf16[8,512,256]{2,1,0:T(8,128)(2,1)}, bf16[8,512,256]{2,1,0:T(8,128)(2,1)S(1)}, u32[]{:S(2)}) copy-start(bf16[8,512,256]{2,1,0:T(8,128)(2,1)S(1)} %subtract_convert_fusion) | copy-start | bytes 6291460
  389.7 6.5 %slice-start.5 = ((s8[9437184]{0:T(1024)(128)(4,1)}), s8[1048576]{0:T(1024)(128)(4,1)S(1)}, s32[]{:S(2)}) async-start(s8[9437184]{0:T(1024)(128)(4,1)} %bitcast.606), calls=%async_computation.10 | async-start | bytes 2097152
  406.0 3.4 copy-start.5
  409.4 186.4 %all-gather.3.cloned.1.call-start = ((), (), s32[]{:S(2)}) async-start(), calls=%async_computation.4 | async-start | bytes 9437184 | tf_op jit(solution)/shard_map/all_gather | solution.py:19
  503.7 6.7 %copy-start.2 = (bf16[8,512,512]{2,1,0:T(8,128)(2,1)S(1)}, bf16[8,512,512]{2,1,0:T(8,128)(2,1)}, u32[]{:S(2)}) copy-start(bf16[8,512,512]{2,1,0:T(8,128)(2,1)} %copy-done.1) | copy-start | bytes 12582916
  503.7 8.6 %copy-start.4 = (bf16[8,512,256]{2,1,0:T(8,128)(2,1)S(1)}, bf16[8,512,256]{2,1,0:T(8,128)(2,1)}, u32[]{:S(2)}) copy-start(bf16[8,512,256]{2,1,0:T(8,128)(2,1)} %copy-done.3) | copy-start | bytes 6291460
Sparse Core Ops, SparseCore 0:
  15.2 187.3 all-reduce.2
  232.0 150.0 all-reduce.4
  409.6 94.1 reduce-scatter.1
  505.2 90.5 all-gather.2
where the time goes:
time: 626 us; the launch traced here: 620 us
  waiting for transfers between devices  316 us (50%)
  other arithmetic  157 us (25%)
  matrix products  99 us (16%)
  local copies, waits for them, and re-layouts  32.2 us (5%)
  between operations  14.7 us (2%)
    psum x1, waiting for transfers between devices, on_device(): complete = lax.psum(rebuilt, 'lat')  150 us
    reduce_or x1, other arithmetic, on_device(): jnp.any(active[source][:, :, None] == columns[None, None, :], axis=1)  142 us
    reduce_scatter x1, waiting for transfers between devices, sum_by_parts(): lax.psum_scatter(padded_to(lines, lax.axis_size(axis)), axis, scatter_dim...  94 us
    all_gather x1, waiting for transfers between devices, sum_by_parts(): whole = lax.all_gather(own, axis).reshape(-1, *lines.shape[1:])  49.8 us
    dot_general x36, matrix products, on_device(): lax.dot_general(latent_act[source], errors[target], by_tokens, preferred_...  42.3 us
    psum x1, waiting for transfers between devices, on_device(): preact = lax.psum(partial_value, 'layer') + bias[:, None, :]  22.3 us
    unnamed x36, local copies, waits for them, and re-layouts  19.8 us
    dot_general x28, matrix products, on_device(): jnp.dot(latent_act[source], decoder[pair_index(source, target)], preferre...  13.8 us
  transfers between devices with their start and end apart: 4, of which 4 were waited for; matrix products, arithmetic and copies ran while one was open for 33% of the time, Pallas kernels for 0%

commit v1 on v0

--- a/solution.py
+++ b/solution.py
@@ -37,7 +37,7 @@
     partial_value = jnp.einsum(
         "ltd,ldf->ltf", activations, encoder, preferred_element_type=jnp.float32
     )
-    preact = lax.psum(partial_value, "layer") + bias[:, None, :]
+    preact = jnp.sum(lax.all_gather(partial_value, axis_name="layer"), axis=0) + bias[:, None, :]
     latent_act = (preact * masks).astype(jnp.bfloat16)
     rebuilt_list = []
     for target in range(LAYERS):

time: 626 us -> 1110 us (1.77)
  waiting for transfers between devices: 316 us -> 776 us
  other arithmetic: 157 us -> 182 us
    all_gather x0 -> x1, waiting for transfers between devices: none -> 482 us  [on_device(): lax.all_gather(partial_value, axis_name='layer')]
    reduce_sum x0 -> x1, other arithmetic: none -> 25.4 us  [on_device(): jnp.sum(lax.all_gather(partial_value, axis_name='layer'), axis=0)]
    psum x1 -> x0, waiting for transfers between devices: 22.3 us -> none  [on_device(): preact = lax.psum(partial_value, 'layer') + bias[:, None, :]]
  transfers between devices with their start and end apart: 4 -> 4, of which waited for: 4 -> 4; matrix products, arithmetic and copies ran while one was open for 33% -> 19% of each run, Pallas kernels for 0% -> 0%
where the time goes in v1:
time: 1110 us; the launch traced here: 1100 us
  waiting for transfers between devices  776 us (70%)
  other arithmetic  182 us (16%)
  matrix products  99.2 us (9%)
  local copies, waits for them, and re-layouts  31.5 us (3%)
  between operations  14.7 us (1%)
    all_gather x1, waiting for transfers between devices, on_device(): lax.all_gather(partial_value, axis_name='layer')  482 us
    psum x1, waiting for transfers between devices, on_device(): complete = lax.psum(rebuilt, 'lat')  150 us
    reduce_or x1, other arithmetic, on_device(): jnp.any(active[source][:, :, None] == columns[None, None, :], axis=1)  141 us
    reduce_scatter x1, waiting for transfers between devices, sum_by_parts(): lax.psum_scatter(padded_to(lines, lax.axis_size(axis)), axis, scatter_dim...  93.9 us
    all_gather x1, waiting for transfers between devices, sum_by_parts(): whole = lax.all_gather(own, axis).reshape(-1, *lines.shape[1:])  49.8 us
    dot_general x36, matrix products, on_device(): lax.dot_general(latent_act[source], errors[target], by_tokens, preferred_...  42.2 us
    reduce_sum x1, other arithmetic, on_device(): jnp.sum(lax.all_gather(partial_value, axis_name='layer'), axis=0)  25.4 us
  transfers between devices with their start and end apart: 4, of which 4 were waited for; matrix products, arithmetic and copies ran while one was open for 19% of the time, Pallas kernels for 0%

profile of v1, /device:TPU:1, one launch (start us, length us, event | category | flops | bytes accessed | tf_op | source)
XLA Modules:
  0.0 1103.4 jit_solution(11333060449312312756)
XLA Ops:
  7.2 1.5 copy-done
  8.8 6.2 fusion.261
  15.1 1.1 copy-done.6
  18.4 1.7 copy.41
  20.1 1.7 copy.40
  21.8 1.7 copy.39
  23.6 1.7 copy.45
  26.2 141.1 %compare_reduce_fusion = (pred[512,512]{1,0:T(8,128)(4,1)S(1)}, pred[512,512]{1,0:T(8,128)(4,1)}, pred[512,512]{1,0:T(8,128)(4,1)}, pred[512,512]{1,0:T(8,128)(4...) fusion(s32[512,64]{1,0:T(8,128)} %copy.45, ...), kind=kLoop, calls=%fused_computation | loop fusion | flops 266338304 | bytes 3147776 | tf_op jit(solution)/shard_map/reduce_or | solution.py:33
  167.3 1.7 bitcast_dynamic-update-slice_fusion.7
  169.0 1.7 bitcast_dynamic-update-slice_fusion.6
  170.6 1.7 bitcast_dynamic-update-slice_fusion.5
  172.3 1.7 bitcast_dynamic-update-slice_fusion.4
  174.0 1.7 bitcast_dynamic-update-slice_fusion.3
  175.7 1.7 bitcast_dynamic-update-slice_fusion.2
  178.8 481.9 %all-gather.5.cloned.1.call-done = f32[64,512,512]{2,1,0:T(8,128)} async-done(((f32[8,512,512]{2,1,0:T(8,128)}), f32[64,512,512]{2,1,0:T(8,128)}) %all-gather.5.cloned.1.call-update) | async-done | bytes 67108880 | tf_op jit(solution)/shard_map/all_gather | solution.py:40
  660.7 25.4 %reduce_sum.18 = f32[8,512,512]{2,1,0:T(8,128)} reduce(f32[8,8,512,512]{3,2,1,0:T(8,128)} %bitcast.16, f32[]{:T(128)} %constant.12.clone.1), dimensions={0}, to_apply=%region_8.0 | reduce | flops 14680064 | bytes 75497472 | tf_op jit(solution)/shard_map/reduce_sum | solution.py:40
  686.1 5.9 select_convert_fusion.1
  692.0 1.5 fusion.183
  693.5 1.4 fusion.177
  695.0 1.2 fusion.169
  696.3 1.2 fusion.159
  697.5 1.2 fusion.147
  698.8 1.2 fusion.133
  700.4 1.1 fusion.15
  707.8 1.1 fusion.29
  708.9 1.1 fusion.27
  710.0 1.1 fusion.25
  711.1 1.1 fusion.23
  712.2 1.1 fusion.21
  713.3 1.1 fusion.19
  714.4 1.1 fusion.17
  715.7 149.9 %all-reduce.2.cloned.1.call-done = f32[8,512,256]{2,1,0:T(8,128)} async-done(((f32[8,512,256]{2,1,0:T(8,128)}), f32[8,512,256]{2,1,0:T(8,128)}) %all-reduce.2.cloned.1.call-update) | async-done | bytes 4194320 | tf_op jit(solution)/shard_map/psum | solution.py:55
  865.6 3.5 subtract_convert_fusion
  869.1 2.8 fusion.119
  871.9 1.3 fusion.135
  873.2 1.4 fusion.149
  874.6 1.3 fusion.161
  875.9 1.3 fusion.171
  877.2 1.3 fusion.179
  878.5 1.3 fusion.185
  889.6 3.4 copy-done.5
  893.2 93.9 %reduce-scatter.2.cloned.1.call-done = f32[512,512]{1,0:T(8,128)} async-done(((f32[4096,512]{1,0:T(8,128)}), f32[512,512]{1,0:T(8,128)}) %reduce-scatter.2.cloned.1.call-update) | async-done | bytes 1048592 | tf_op jit(solution)/shard_map/reduce_scatter | solution.py:16
  987.2 2.3 fusion.31
  989.5 2.2 fusion.33
  991.7 2.2 fusion.35
  993.9 2.0 fusion.37
  995.9 1.1 fusion.39
  996.9 1.1 fusion.41
  998.0 1.1 fusion.43
  1003.2 1.1 fusion.53
  1004.3 1.1 fusion.55
  1008.5 1.1 fusion.63
  1009.5 1.1 fusion.65
  1010.6 1.1 fusion.67
  1015.8 1.1 fusion.77
  1016.9 1.1 fusion.79
  1021.1 1.1 fusion.87
  1022.1 1.1 fusion.89
  1023.2 1.1 fusion.91
  1028.4 1.1 fusion.101
  1029.5 49.8 %all-gather.7.cloned.1.call-done = f32[4096,512]{1,0:T(8,128)} async-done(((f32[512,512]{1,0:T(8,128)}), f32[4096,512]{1,0:T(8,128)}) %all-gather.7.cloned.1.call-update) | async-done | bytes 8388624 | tf_op jit(solution)/shard_map/all_gather | solution.py:19
  1079.3 7.5 convert_bitcast_fusion
  1086.7 3.9 copy.47
  1090.6 6.0 convert_reduce_fusion
  (112 shorter events, 40.0 us)
Async XLA Ops:
  7.2 1.6 copy-start
  7.2 653.5 %all-gather.5.cloned.1.call-start = ((), (), s32[]{:S(2)}) async-start(), calls=%async_computation.3 | async-start | bytes 75497472 | tf_op jit(solution)/shard_map/all_gather | solution.py:40
  15.0 1.2 copy-start.6
  15.0 850.6 %all-reduce.2.cloned.1.call-start = ((), (), s32[]{:S(2)}) async-start(), calls=%async_computation.1 | async-start | bytes 8388608 | tf_op jit(solution)/shard_map/psum | solution.py:55
  660.7 25.4 %copy-start.7 = (f32[8,512]{1,0:T(8,128)S(1)}, f32[8,512]{1,0:T(8,128)}, u32[]{:S(2)}) copy-start(f32[8,512]{1,0:T(8,128)} %param.9) | copy-start | bytes 49156
  686.1 14.0 %slice-start = ((s8[9437184]{0:T(1024)(128)(4,1)}), s8[4194304]{0:T(1024)(128)(4,1)S(1)}, s32[]{:S(2)}) async-start(s8[9437184]{0:T(1024)(128)(4,1)} %bitcast.605), calls=%async_computation.5 | async-start | bytes 8388608
  686.1 14.0 %slice-start.1 = ((s8[9437184]{0:T(1024)(128)(4,1)}), s8[4194304]{0:T(1024)(128)(4,1)S(1)}, s32[]{:S(2)}) async-start(s8[9437184]{0:T(1024)(128)(4,1)} %bitcast.605), calls=%async_computation.6 | async-start | bytes 8388608
  692.0 22.4 %copy-start.1 = (bf16[8,512,512]{2,1,0:T(8,128)(2,1)}, bf16[8,512,512]{2,1,0:T(8,128)(2,1)S(1)}, u32[]{:S(2)}) copy-start(bf16[8,512,512]{2,1,0:T(8,128)(2,1)S(1)} %select_convert_fusion.1) | copy-start | bytes 12582916
  692.0 8.0 slice-start.2
  715.5 271.7 %reduce-scatter.2.cloned.1.call-start = ((), (), s32[]{:S(2)}) async-start(), calls=%async_computation.2 | async-start | bytes 9437184 | tf_op jit(solution)/shard_map/reduce_scatter | solution.py:16
  865.6 14.1 %slice-start.3 = ((s8[9437184]{0:T(1024)(128)(4,1)}), s8[4194304]{0:T(1024)(128)(4,1)S(1)}, s32[]{:S(2)}) async-start(s8[9437184]{0:T(1024)(128)(4,1)} %bitcast.607), calls=%async_computation.8 | async-start | bytes 8388608
  865.6 14.2 %slice-start.4 = ((s8[9437184]{0:T(1024)(128)(4,1)}), s8[4194304]{0:T(1024)(128)(4,1)S(1)}, s32[]{:S(2)}) async-start(s8[9437184]{0:T(1024)(128)(4,1)} %bitcast.607), calls=%async_computation.9 | async-start | bytes 8388608
  869.1 20.1 %copy-start.3 = (bf16[8,512,256]{2,1,0:T(8,128)(2,1)}, bf16[8,512,256]{2,1,0:T(8,128)(2,1)S(1)}, u32[]{:S(2)}) copy-start(bf16[8,512,256]{2,1,0:T(8,128)(2,1)S(1)} %subtract_convert_fusion) | copy-start | bytes 6291460
  873.2 6.5 slice-start.5
  889.6 3.4 copy-start.5
  893.0 186.3 %all-gather.7.cloned.1.call-start = ((), (), s32[]{:S(2)}) async-start(), calls=%async_computation.4 | async-start | bytes 9437184 | tf_op jit(solution)/shard_map/all_gather | solution.py:19
  987.2 6.7 copy-start.2
  987.2 8.6 copy-start.4
Sparse Core Ops, SparseCore 0:
  15.2 645.4 all-gather.4
  715.6 149.9 all-reduce.1
  893.1 94.0 reduce-scatter.1
  988.7 90.5 all-gather.6
